TPU v7x, 256 devices: a whole 4x4x8 slice. The times are simulated.
256 devices in a mesh: patch: 32 (over z, y_lo, core), lag: 8 (over x, y_hi).
Axes of the slice: x: 4, y: 4 (y_hi: 2, y_lo: 2; y = y_hi * 2 + y_lo), z: 8, core: 2. Of those that a mesh axis runs over, the one named last changes fastest.
Arguments:
- interaction: bfloat16 [120, 8192, 1280], P('lag', 'patch'), may hold values from -0.0234375 to 0.0234375
- history: bfloat16 [120, 8192, 128], P('lag', 'patch'), may hold values from -6 to 6
- near_inverse: bfloat16 [8192, 256], P('patch'), may hold values from -0.375 to 0.375
- lag_ranges: int32 [32, 10], P('patch'), may hold values from 1 to 121, as said below
- receiver_tile: int32 [8192, 1], P('patch'), may hold values from 0 to 31; in each aligned block of 256 rows (0 to 255, 256 to 511, ...) at most 16 rows name the same one
- receiver_panel: int32 [8192], P('patch'), may hold values from 0 to 255
- residuals: bfloat16 [8192, 4, 128], P('patch'), may hold values from -6 to 6
Outputs:
- densities: bfloat16 [4, 8192, 128], P(None, 'patch')
Inputs may be any that keep to these rules, and one draw needn't show every extreme that they name: `lag_ranges`: columns 0 to 4 hold the first active lag, columns 5 to 9 one past the last; every range holds at least 30 lags. `receiver_tile`: among the 256 receivers of one patch index, at most 16 lie on one patch.
All inputs are finite; a program needn't handle non-finite values.
Results may differ from a plain program's by a relative error of at most 0.0049.
Values may be sent and summed in bfloat16 or wider, within the bound.
A program may use at most 64 MiB of HBM per device.

v0:
```python
import jax
import jax.numpy as jnp
from jax import lax
from jax.sharding import PartitionSpec as P

NEAR = 5
CAP = 16


def side_by_side(arrays, axis, split_dim, concat_dim, along):
    ends, at = ([], 0)
    for a in arrays[:-1]:
        at += a.shape[along]
        ends.append(at)
    both = jnp.concatenate(arrays, axis=along)
    return tuple(
        jnp.split(
            lax.all_to_all(both, axis, split_axis=split_dim, concat_axis=concat_dim, tiled=True),
            ends,
            axis=along,
        )
    )


def from_behind(block, axis, distance):
    devices = range(lax.axis_size(axis))
    route = [(i - distance, i) for i in devices if i - distance in devices]
    return lax.ppermute(block, axis, route)


def from_behind_2(shard, axis, by):
    devices = lax.axis_size(axis)
    return lax.ppermute(shard, axis, [(i, (i + by) % devices) for i in range(devices)])


def sent_to_all(shard, axis):
    copies = jnp.broadcast_to(shard, (lax.axis_size(axis), *shard.shape))
    return lax.all_to_all(copies, axis, split_axis=0, concat_axis=0, tiled=True)


def taken_together(shard, axis):
    return sent_to_all(shard, axis).sum(axis=0)


def contract_rows(block_cols, masked):
    return lax.dot_general(
        block_cols, masked, (((0,), (0,)), ((), ())), preferred_element_type=jnp.float32
    )


def local(interaction, history, near_inverse, lag_ranges, receiver_tile, receiver_panel, residuals):
    tile_len = near_inverse.shape[1]
    band_len = history.shape[0]
    shot_len = history.shape[2]
    step_count = residuals.shape[1]
    half_near = NEAR // 2
    patches = lax.axis_size("patch")
    recv_count = residuals.shape[0]
    target = receiver_tile[:, 0]
    by_target = (target[:, None] == jnp.arange(patches, dtype=jnp.int32)[None, :]).astype(jnp.int32)
    earlier_same = jnp.sum((jnp.cumsum(by_target, 0) - by_target) * by_target, 1)
    slot_index = target * CAP + earlier_same
    placer = (slot_index[:, None] == jnp.arange(patches * CAP, dtype=jnp.int32)[None, :]).astype(
        jnp.bfloat16
    )
    flat_rows = residuals.reshape(recv_count, step_count * shot_len)
    outgoing = lax.dot_general(
        placer, flat_rows, (((0,), (0,)), ((), ())), preferred_element_type=jnp.float32
    ).astype(jnp.bfloat16)
    panel_marks = (receiver_panel + 1).astype(jnp.bfloat16)[:, None]
    labels = lax.dot_general(
        placer, panel_marks, (((0,), (0,)), ((), ())), preferred_element_type=jnp.float32
    ).astype(jnp.bfloat16)
    arrived, arrived_labels = side_by_side((outgoing, labels), "patch", 0, 0, 1)
    panel_ids = (jnp.arange(tile_len, dtype=jnp.int32) + 1).astype(jnp.bfloat16)
    picker = (arrived_labels[:, 0][None, :] == panel_ids[:, None]).astype(jnp.bfloat16)
    source = jnp.dot(picker, arrived, preferred_element_type=jnp.float32).reshape(
        tile_len, step_count, shot_len
    )
    rim_rows = from_behind(history[band_len - step_count + 1 :], "lag", 1)
    is_first = lax.axis_index("lag") == 0
    extended = jnp.concatenate([rim_rows, history], 0)
    lag_numbers = lax.axis_index("lag") * band_len + jnp.arange(band_len, dtype=jnp.int32) + 1
    lower = lag_ranges[0, :NEAR]
    upper = lag_ranges[0, NEAR:]
    active = (
        (lag_numbers[:, None] >= lower[None, :]) & (lag_numbers[:, None] < upper[None, :])
    ).astype(jnp.bfloat16)
    weights = interaction.reshape(band_len * tile_len, NEAR * tile_len)
    results = []
    for step_idx in range(step_count):
        start_row = step_count - 1 - step_idx
        window = extended[start_row : start_row + band_len]
        terms = []
        for offset in range(NEAR):
            masked = (window * active[:, offset][:, None, None]).reshape(
                band_len * tile_len, shot_len
            )
            terms.append(
                contract_rows(weights[:, offset * tile_len : (offset + 1) * tile_len], masked)
            )
        contrib = jnp.stack(terms)
        incoming = contrib[half_near]
        for offset in range(NEAR):
            if offset != half_near:
                incoming = incoming + from_behind_2(contrib[offset], "patch", offset - half_near)
        totals = taken_together(incoming, "lag")
        right_side = (source[:, step_idx] - totals).astype(jnp.bfloat16)
        density = lax.dot_general(
            near_inverse, right_side, (((0,), (0,)), ((), ())), preferred_element_type=jnp.float32
        ).astype(jnp.bfloat16)
        results.append(density)
        if step_idx < step_count - 1:
            slot_row = step_count - 2 - step_idx
            extended = extended.at[slot_row].set(jnp.where(is_first, density, extended[slot_row]))
    return jnp.stack(results)


def solution(mesh):
    in_specs = (
        P("lag", "patch", None),
        P("lag", "patch", None),
        P("patch", None),
        P("patch", None),
        P("patch", None),
        P("patch"),
        P("patch", None, None),
    )
    out_specs = P(None, "patch", None)
    return jax.shard_map(local, mesh=mesh, in_specs=in_specs, out_specs=out_specs, check_vma=False)
```

profile of v0, /device:TPU:1, one launch (start us, length us, event | category | flops | bytes accessed | tf_op | source)
XLA Modules:
  0.0 248.3 jit_solution(9878374172398110391)
XLA Ops:
  6.6 3.0 %fusion.64 = f32[256,128]{0,1:T(8,128)} fusion(bf16[3840,128]{1,0:T(8,128)(2,1)} %bitcast.250, bf16[3840,1280]{1,0:T(8,128)(2,1)} %bitcast.226), kind=kOutput, calls=%fused_computation.50 | convolution fusion | flops 251658240 | bytes 3080192 | tf_op jit(solution)/shard_map/dot_general | solution.py:46
  9.6 7.4 %collective-permute-start = (f32[256,128]{0,1:T(8,128)}, f32[256,128]{0,1:T(8,128)}, u32[]{:S(2)}, u32[]{:S(2)}) collective-permute-start(f32[256,128]{0,1:T(8,128)} %fusion.64), channel_id=1, source_target_pairs={{0,240},{8,248},{16,0},{24,8},{32,16},{40,24},{48,32},{56,40},{64,... | collective-permute-start | bytes 393224 | tf_op jit(solution)/shard_map/ppermute | solution.py:33
  19.3 3.1 %fusion.76 = f32[256,128]{0,1:T(8,128)} fusion(bf16[3840,128]{1,0:T(8,128)(2,1)} %bitcast.251, bf16[3840,1280]{1,0:T(8,128)(2,1)} %bitcast.227), kind=kOutput, calls=%fused_computation.54 | convolution fusion | flops 251658240 | bytes 3080192 | tf_op jit(solution)/shard_map/dot_general | solution.py:46
  28.0 4.4 %all-to-all-start = ((bf16[32,16,513]{2,1,0:T(8,128)(2,1)}), bf16[32,16,513]{2,1,0:T(8,128)(2,1)}, u32[]{:S(2)}, u32[]{:S(2)}) async-start(bf16[32,16,513]{2,1,0:T(8,128)(2,1)} %pad_maximum_fusion.1), calls=%async_computation | async-start | bytes 1310720 | tf_op jit(solution)/shard_map/all_to_all | solution.py:18
  34.7 3.0 %fusion.88 = f32[256,128]{0,1:T(8,128)} fusion(bf16[3840,128]{1,0:T(8,128)(2,1)} %bitcast.252, bf16[3840,1280]{1,0:T(8,128)(2,1)} %bitcast.228), kind=kOutput, calls=%fused_computation.58 | convolution fusion | flops 251658240 | bytes 3080192 | tf_op jit(solution)/shard_map/dot_general | solution.py:46
  40.5 3.0 %fusion.100 = f32[256,128]{0,1:T(8,128)} fusion(bf16[3840,128]{1,0:T(8,128)(2,1)} %bitcast.253, bf16[3840,1280]{1,0:T(8,128)(2,1)} %bitcast.229), kind=kOutput, calls=%fused_computation.62 | convolution fusion | flops 251658240 | bytes 3080192 | tf_op jit(solution)/shard_map/dot_general | solution.py:46
  44.8 4.5 %collective-permute-start.4 = (bf16[3,256,128]{1,2,0:T(8,128)(2,1)S(1)}, bf16[3,256,128]{1,2,0:T(8,128)(2,1)S(1)}, u32[]{:S(2)}, u32[]{:S(2)}) collective-permute-start(bf16[3,256,128]{1,2,0:T(8,128)(2,1)S(1)} %slice.198), channel_id=1, source_target_pairs={{0,1},{1,2},{2,3},{3,4},{4,5},{5,6},{6,7},{8,9},{9,10},{10,11},{11... | collective-permute-start | bytes 589832 | tf_op jit(solution)/shard_map/ppermute | solution.py:28
  50.1 5.1 %collective-permute-done.3 = f32[256,128]{0,1:T(8,128)} collective-permute-done((f32[256,128]{0,1:T(8,128)}, f32[256,128]{0,1:T(8,128)}, u32[]{:S(2)}, u32[]{:S(2)}) %collective-permute-start.3) | collective-permute-done | bytes 131104 | tf_op jit(solution)/shard_map/ppermute | solution.py:33
  58.7 8.7 %all-to-all-start.1 = ((f32[8,256,128]{2,1,0:T(8,128)}), f32[8,256,128]{2,1,0:T(8,128)S(1)}, u32[]{:S(2)}, u32[]{:S(2)}) async-start(f32[8,256,128]{2,1,0:T(8,128)} %broadcast_in_dim.8), calls=%async_computation.1 | async-start | bytes 2097152 | tf_op jit(solution)/shard_map/all_to_all | solution.py:38
  73.1 11.9 %all-to-all-done.1 = f32[8,256,128]{2,1,0:T(8,128)S(1)} async-done(((f32[8,256,128]{2,1,0:T(8,128)}), f32[8,256,128]{2,1,0:T(8,128)S(1)}, u32[]{:S(2)}, u32[]{:S(2)}) %all-to-all-start.1) | async-done | bytes 1048608 | tf_op jit(solution)/shard_map/all_to_all | solution.py:38
  90.1 3.0 %fusion.67 = f32[256,128]{0,1:T(8,128)} fusion(bf16[3840,128]{1,0:T(8,128)(2,1)} %bitcast.254, bf16[3840,1280]{1,0:T(8,128)(2,1)} %bitcast.231), kind=kOutput, calls=%fused_computation.51 | convolution fusion | flops 251658240 | bytes 3080192 | tf_op jit(solution)/shard_map/dot_general | solution.py:46
  95.4 3.0 %fusion.79 = f32[256,128]{0,1:T(8,128)} fusion(bf16[3840,128]{1,0:T(8,128)(2,1)} %bitcast.255, bf16[3840,1280]{1,0:T(8,128)(2,1)} %bitcast.232), kind=kOutput, calls=%fused_computation.55 | convolution fusion | flops 251658240 | bytes 3080192 | tf_op jit(solution)/shard_map/dot_general | solution.py:46
  101.1 3.0 %fusion.91 = f32[256,128]{0,1:T(8,128)} fusion(bf16[3840,128]{1,0:T(8,128)(2,1)} %bitcast.256, bf16[3840,1280]{1,0:T(8,128)(2,1)} %bitcast.233), kind=kOutput, calls=%fused_computation.59 | convolution fusion | flops 251658240 | bytes 3080192 | tf_op jit(solution)/shard_map/dot_general | solution.py:46
  107.1 3.0 %fusion.103 = f32[256,128]{0,1:T(8,128)} fusion(bf16[3840,128]{1,0:T(8,128)(2,1)} %bitcast.257, bf16[3840,1280]{1,0:T(8,128)(2,1)} %bitcast.234), kind=kOutput, calls=%fused_computation.63 | convolution fusion | flops 251658240 | bytes 3080192 | tf_op jit(solution)/shard_map/dot_general | solution.py:46
  113.0 5.6 %collective-permute-done.8 = f32[256,128]{0,1:T(8,128)} collective-permute-done((f32[256,128]{0,1:T(8,128)}, f32[256,128]{0,1:T(8,128)}, u32[]{:S(2)}, u32[]{:S(2)}) %collective-permute-start.8) | collective-permute-done | bytes 131104 | tf_op jit(solution)/shard_map/ppermute | solution.py:33
  121.1 19.4 %all_to_all.29 = f32[8,256,128]{2,1,0:T(8,128)S(1)} all-to-all(f32[8,256,128]{2,1,0:T(8,128)S(1)} %broadcast_in_dim.9), channel_id=1, replica_groups=mesh['patch'=32,'lag'=8] {'lag'}, dimensions={0} | all-to-all | bytes 2097152 | tf_op jit(solution)/shard_map/all_to_all | solution.py:38
  140.8 2.4 slice_multiply_fusion.9
  145.4 3.0 %fusion.82 = f32[256,128]{0,1:T(8,128)} fusion(bf16[3840,128]{1,0:T(8,128)(2,1)} %bitcast.258, bf16[3840,1280]{1,0:T(8,128)(2,1)} %bitcast.236), kind=kOutput, calls=%fused_computation.56 | convolution fusion | flops 251658240 | bytes 3080192 | tf_op jit(solution)/shard_map/dot_general | solution.py:46
  148.5 2.5 collective-permute-start.10
  153.2 3.0 %fusion.94 = f32[256,128]{0,1:T(8,128)} fusion(bf16[3840,128]{1,0:T(8,128)(2,1)} %bitcast.259, bf16[3840,1280]{1,0:T(8,128)(2,1)} %bitcast.237), kind=kOutput, calls=%fused_computation.60 | convolution fusion | flops 251658240 | bytes 3080192 | tf_op jit(solution)/shard_map/dot_general | solution.py:46
  158.4 3.0 %fusion.106 = f32[256,128]{0,1:T(8,128)} fusion(bf16[3840,128]{1,0:T(8,128)(2,1)} %bitcast.260, bf16[3840,1280]{1,0:T(8,128)(2,1)} %bitcast.238), kind=kOutput, calls=%fused_computation.64 | convolution fusion | flops 251658240 | bytes 3080192 | tf_op jit(solution)/shard_map/dot_general | solution.py:46
  162.8 3.0 %fusion.70 = f32[256,128]{0,1:T(8,128)} fusion(bf16[3840,128]{1,0:T(8,128)(2,1)} %bitcast.261, bf16[3840,1280]{1,0:T(8,128)(2,1)} %bitcast.239), kind=kOutput, calls=%fused_computation.52 | convolution fusion | flops 251658240 | bytes 3080192 | tf_op jit(solution)/shard_map/dot_general | solution.py:46
  165.9 3.6 %collective-permute-start.9 = (f32[256,128]{0,1:T(8,128)}, f32[256,128]{0,1:T(8,128)}, u32[]{:S(2)}, u32[]{:S(2)}) collective-permute-start(f32[256,128]{0,1:T(8,128)} %fusion.70), channel_id=1, source_target_pairs={{0,240},{8,248},{16,0},{24,8},{32,16},{40,24},{48,32},{56,40},{64,... | collective-permute-start | bytes 393224 | tf_op jit(solution)/shard_map/ppermute | solution.py:33
  174.3 16.8 %all_to_all.30 = f32[8,256,128]{2,1,0:T(8,128)S(1)} all-to-all(f32[8,256,128]{2,1,0:T(8,128)S(1)} %broadcast_in_dim.10), channel_id=1, replica_groups=mesh['patch'=32,'lag'=8] {'lag'}, dimensions={0} | all-to-all | bytes 2097152 | tf_op jit(solution)/shard_map/all_to_all | solution.py:38
  192.0 2.4 slice_multiply_fusion.4
  196.7 3.1 %fusion.73 = f32[256,128]{0,1:T(8,128)} fusion(bf16[3840,128]{1,0:T(8,128)(2,1)} %bitcast.262, bf16[3840,1280]{1,0:T(8,128)(2,1)} %bitcast.241), kind=kOutput, calls=%fused_computation.53 | convolution fusion | flops 251658240 | bytes 3080192 | tf_op jit(solution)/shard_map/dot_general | solution.py:46
  199.8 4.9 %collective-permute-start.13 = (f32[256,128]{0,1:T(8,128)}, f32[256,128]{0,1:T(8,128)S(1)}, u32[]{:S(2)}, u32[]{:S(2)}) collective-permute-start(f32[256,128]{0,1:T(8,128)} %fusion.73), channel_id=1, source_target_pairs={{0,240},{8,248},{16,0},{24,8},{32,16},{40,24},{48,32},{56,40},{64,... | collective-permute-start | bytes 393224 | tf_op jit(solution)/shard_map/ppermute | solution.py:33
  206.1 3.1 %fusion.85 = f32[256,128]{0,1:T(8,128)} fusion(bf16[3840,128]{1,0:T(8,128)(2,1)} %bitcast.263, bf16[3840,1280]{1,0:T(8,128)(2,1)} %bitcast.242), kind=kOutput, calls=%fused_computation.57 | convolution fusion | flops 251658240 | bytes 3080192 | tf_op jit(solution)/shard_map/dot_general | solution.py:46
  209.2 3.1 %collective-permute-start.14 = (f32[256,128]{0,1:T(8,128)}, f32[256,128]{0,1:T(8,128)}, u32[]{:S(2)}, u32[]{:S(2)}) collective-permute-start(f32[256,128]{0,1:T(8,128)} %fusion.85), channel_id=1, source_target_pairs={{0,248},{8,0},{16,8},{24,16},{32,24},{40,32},{48,40},{56,48},{64,5... | collective-permute-start | bytes 393224 | tf_op jit(solution)/shard_map/ppermute | solution.py:33
  213.6 3.0 %fusion.97 = f32[256,128]{0,1:T(8,128)} fusion(bf16[3840,128]{1,0:T(8,128)(2,1)} %bitcast.264, bf16[3840,1280]{1,0:T(8,128)(2,1)} %bitcast.243), kind=kOutput, calls=%fused_computation.61 | convolution fusion | flops 251658240 | bytes 3080192 | tf_op jit(solution)/shard_map/dot_general | solution.py:46
  220.4 5.8 %collective-permute-done.16 = f32[256,128]{0,1:T(8,128)S(1)} collective-permute-done((f32[256,128]{0,1:T(8,128)S(1)}, f32[256,128]{0,1:T(8,128)S(1)}, u32[]{:S(2)}, u32[]{:S(2)}) %collective-permute-start.16) | collective-permute-done | bytes 131104 | tf_op jit(solution)/shard_map/ppermute | solution.py:33
  228.6 18.6 %all_to_all.31 = f32[8,256,128]{2,1,0:T(8,128)S(1)} all-to-all(f32[8,256,128]{2,1,0:T(8,128)S(1)} %broadcast_in_dim.22), channel_id=1, replica_groups=mesh['patch'=32,'lag'=8] {'lag'}, dimensions={0} | all-to-all | bytes 2097152 | tf_op jit(solution)/shard_map/all_to_all | solution.py:38
  (123 shorter events, 75.0 us)
Async XLA Ops:
  0.0 85.0 %copy-start = (bf16[256,256]{1,0:T(8,128)(2,1)S(1)}, bf16[256,256]{1,0:T(8,128)(2,1)}, u32[]{:S(2)}) copy-start(bf16[256,256]{1,0:T(8,128)(2,1)} %param.15) | copy-start | bytes 393220
  0.9 3.4 %copy-start.9 = (bf16[15]{0:T(256)(128)(2,1)}, bf16[15]{0:T(256)(128)(2,1)S(1)}, u32[]{:S(2)}) copy-start(bf16[15]{0:T(256)(128)(2,1)S(1)} %get-tuple-element.69) | copy-start | bytes 94
  9.6 40.5 %collective-permute-start = (f32[256,128]{0,1:T(8,128)}, f32[256,128]{0,1:T(8,128)}, u32[]{:S(2)}, u32[]{:S(2)}) collective-permute-start(f32[256,128]{0,1:T(8,128)} %fusion.64), channel_id=1, source_target_pairs={{0,240},{8,248},{16,0},{24,8},{32,16},{40,24},{48,32},{56,40},{64,... | collective-permute-start | bytes 393224 | tf_op jit(solution)/shard_map/ppermute | solution.py:33
  19.2 4.0 %copy-start.11 = (s32[256,1]{0,1:T(1,128)S(1)}, s32[256,1]{0,1:T(1,128)}, u32[]{:S(2)}) copy-start(s32[256,1]{0,1:T(1,128)} %param.17) | copy-start | bytes 3076
  19.3 5.0 %copy-start.12 = (s32[256]{0:T(256)S(1)}, s32[256]{0:T(256)}, u32[]{:S(2)}) copy-start(s32[256]{0:T(256)} %param.18) | copy-start | bytes 3076
  19.3 5.0 %copy-start.6 = (bf16[256,4,128]{2,1,0:T(4,128)(2,1)S(1)}, bf16[256,4,128]{2,1,0:T(4,128)(2,1)}, u32[]{:S(2)}) copy-start(bf16[256,4,128]{2,1,0:T(4,128)(2,1)} %param.19) | copy-start | bytes 786436
  22.3 27.8 %collective-permute-start.1 = (f32[256,128]{0,1:T(8,128)}, f32[256,128]{0,1:T(8,128)}, u32[]{:S(2)}, u32[]{:S(2)}) collective-permute-start(f32[256,128]{0,1:T(8,128)} %fusion.76), channel_id=1, source_target_pairs={{0,248},{8,0},{16,8},{24,16},{32,24},{40,32},{48,40},{56,48},{64,5... | collective-permute-start | bytes 393224 | tf_op jit(solution)/shard_map/ppermute | solution.py:33
  28.0 29.6 %all-to-all-start = ((bf16[32,16,513]{2,1,0:T(8,128)(2,1)}), bf16[32,16,513]{2,1,0:T(8,128)(2,1)}, u32[]{:S(2)}, u32[]{:S(2)}) async-start(bf16[32,16,513]{2,1,0:T(8,128)(2,1)} %pad_maximum_fusion.1), calls=%async_computation | async-start | bytes 1310720 | tf_op jit(solution)/shard_map/all_to_all | solution.py:18
  37.7 12.4 %collective-permute-start.2 = (f32[256,128]{0,1:T(8,128)}, f32[256,128]{0,1:T(8,128)}, u32[]{:S(2)}, u32[]{:S(2)}) collective-permute-start(f32[256,128]{0,1:T(8,128)} %fusion.88), channel_id=1, source_target_pairs={{0,8},{8,16},{16,24},{24,32},{32,40},{40,48},{48,56},{56,64},{64,7... | collective-permute-start | bytes 393224 | tf_op jit(solution)/shard_map/ppermute | solution.py:33
  43.5 11.7 %collective-permute-start.3 = (f32[256,128]{0,1:T(8,128)}, f32[256,128]{0,1:T(8,128)}, u32[]{:S(2)}, u32[]{:S(2)}) collective-permute-start(f32[256,128]{0,1:T(8,128)} %fusion.100), channel_id=1, source_target_pairs={{0,16},{8,24},{16,32},{24,40},{32,48},{40,56},{48,64},{56,72},{64,... | collective-permute-start | bytes 393224 | tf_op jit(solution)/shard_map/ppermute | solution.py:33
  44.8 22.6 %collective-permute-start.4 = (bf16[3,256,128]{1,2,0:T(8,128)(2,1)S(1)}, bf16[3,256,128]{1,2,0:T(8,128)(2,1)S(1)}, u32[]{:S(2)}, u32[]{:S(2)}) collective-permute-start(bf16[3,256,128]{1,2,0:T(8,128)(2,1)S(1)} %slice.198), channel_id=1, source_target_pairs={{0,1},{1,2},{2,3},{3,4},{4,5},{5,6},{6,7},{8,9},{9,10},{10,11},{11... | collective-permute-start | bytes 589832 | tf_op jit(solution)/shard_map/ppermute | solution.py:28
  58.7 26.3 %all-to-all-start.1 = ((f32[8,256,128]{2,1,0:T(8,128)}), f32[8,256,128]{2,1,0:T(8,128)S(1)}, u32[]{:S(2)}, u32[]{:S(2)}) async-start(f32[8,256,128]{2,1,0:T(8,128)} %broadcast_in_dim.8), calls=%async_computation.1 | async-start | bytes 2097152 | tf_op jit(solution)/shard_map/all_to_all | solution.py:38
  67.4 3.4 %copy-start.5 = (bf16[3,256,128]{1,2,0:T(8,128)(2,1)}, bf16[3,256,128]{1,2,0:T(8,128)(2,1)S(1)}, u32[]{:S(2)}) copy-start(bf16[3,256,128]{1,2,0:T(8,128)(2,1)S(1)} %collective-permute-done.4) | copy-start | bytes 589828
  72.0 14.1 %copy-start.10 = (bf16[15]{0:T(256)(128)(2,1)S(1)}, bf16[15]{0:T(256)(128)(2,1)}, u32[]{:S(2)}) copy-start(bf16[15]{0:T(256)(128)(2,1)} %copy-done.9) | copy-start | bytes 94
  93.2 19.8 %collective-permute-start.5 = (f32[256,128]{0,1:T(8,128)}, f32[256,128]{0,1:T(8,128)}, u32[]{:S(2)}, u32[]{:S(2)}) collective-permute-start(f32[256,128]{0,1:T(8,128)} %fusion.67), channel_id=1, source_target_pairs={{0,240},{8,248},{16,0},{24,8},{32,16},{40,24},{48,32},{56,40},{64,... | collective-permute-start | bytes 393224 | tf_op jit(solution)/shard_map/ppermute | solution.py:33
  98.4 14.6 %collective-permute-start.6 = (f32[256,128]{0,1:T(8,128)}, f32[256,128]{0,1:T(8,128)}, u32[]{:S(2)}, u32[]{:S(2)}) collective-permute-start(f32[256,128]{0,1:T(8,128)} %fusion.79), channel_id=1, source_target_pairs={{0,248},{8,0},{16,8},{24,16},{32,24},{40,32},{48,40},{56,48},{64,5... | collective-permute-start | bytes 393224 | tf_op jit(solution)/shard_map/ppermute | solution.py:33
  104.1 8.9 %collective-permute-start.7 = (f32[256,128]{0,1:T(8,128)}, f32[256,128]{0,1:T(8,128)}, u32[]{:S(2)}, u32[]{:S(2)}) collective-permute-start(f32[256,128]{0,1:T(8,128)} %fusion.91), channel_id=1, source_target_pairs={{0,8},{8,16},{16,24},{24,32},{32,40},{40,48},{48,56},{56,64},{64,7... | collective-permute-start | bytes 393224 | tf_op jit(solution)/shard_map/ppermute | solution.py:33
  110.1 8.5 %collective-permute-start.8 = (f32[256,128]{0,1:T(8,128)}, f32[256,128]{0,1:T(8,128)}, u32[]{:S(2)}, u32[]{:S(2)}) collective-permute-start(f32[256,128]{0,1:T(8,128)} %fusion.103), channel_id=1, source_target_pairs={{0,16},{8,24},{16,32},{24,40},{32,48},{40,56},{48,64},{56,72},{64,... | collective-permute-start | bytes 393224 | tf_op jit(solution)/shard_map/ppermute | solution.py:33
  121.0 19.6 %copy-start.4 = (f32[256,1,128]{2,1,0:T(1,128)S(1)}, f32[256,1,128]{2,1,0:T(1,128)}, u32[]{:S(2)}) copy-start(f32[256,1,128]{2,1,0:T(1,128)} %get-tuple-element.62) | copy-start | bytes 393220
  148.5 21.7 %collective-permute-start.10 = (f32[256,128]{0,1:T(8,128)}, f32[256,128]{0,1:T(8,128)}, u32[]{:S(2)}, u32[]{:S(2)}) collective-permute-start(f32[256,128]{0,1:T(8,128)} %fusion.82), channel_id=1, source_target_pairs={{0,248},{8,0},{16,8},{24,16},{32,24},{40,32},{48,40},{56,48},{64,5... | collective-permute-start | bytes 393224 | tf_op jit(solution)/shard_map/ppermute | solution.py:33
  156.2 14.0 %collective-permute-start.11 = (f32[256,128]{0,1:T(8,128)}, f32[256,128]{0,1:T(8,128)}, u32[]{:S(2)}, u32[]{:S(2)}) collective-permute-start(f32[256,128]{0,1:T(8,128)} %fusion.94), channel_id=1, source_target_pairs={{0,8},{8,16},{16,24},{24,32},{32,40},{40,48},{48,56},{56,64},{64,7... | collective-permute-start | bytes 393224 | tf_op jit(solution)/shard_map/ppermute | solution.py:33
  161.5 8.8 %collective-permute-start.12 = (f32[256,128]{0,1:T(8,128)}, f32[256,128]{0,1:T(8,128)}, u32[]{:S(2)}, u32[]{:S(2)}) collective-permute-start(f32[256,128]{0,1:T(8,128)} %fusion.106), channel_id=1, source_target_pairs={{0,16},{8,24},{16,32},{24,40},{32,48},{40,56},{48,64},{56,72},{64,... | collective-permute-start | bytes 393224 | tf_op jit(solution)/shard_map/ppermute | solution.py:33
  165.9 6.0 %collective-permute-start.9 = (f32[256,128]{0,1:T(8,128)}, f32[256,128]{0,1:T(8,128)}, u32[]{:S(2)}, u32[]{:S(2)}) collective-permute-start(f32[256,128]{0,1:T(8,128)} %fusion.70), channel_id=1, source_target_pairs={{0,240},{8,248},{16,0},{24,8},{32,16},{40,24},{48,32},{56,40},{64,... | collective-permute-start | bytes 393224 | tf_op jit(solution)/shard_map/ppermute | solution.py:33
  174.2 17.0 %copy-start.3 = (f32[256,1,128]{2,1,0:T(1,128)S(1)}, f32[256,1,128]{2,1,0:T(1,128)}, u32[]{:S(2)}) copy-start(f32[256,1,128]{2,1,0:T(1,128)} %get-tuple-element.61) | copy-start | bytes 393220
  196.7 8.0 %copy-start.2 = (bf16[15,256,128]{1,2,0:T(8,128)(2,1)S(1)}, bf16[15,256,128]{1,2,0:T(8,128)(2,1)}, u32[]{:S(2)}) copy-start(bf16[15,256,128]{1,2,0:T(8,128)(2,1)} %get-tuple-element.43) | copy-start | bytes 2949124
  199.8 20.6 %collective-permute-start.13 = (f32[256,128]{0,1:T(8,128)}, f32[256,128]{0,1:T(8,128)S(1)}, u32[]{:S(2)}, u32[]{:S(2)}) collective-permute-start(f32[256,128]{0,1:T(8,128)} %fusion.73), channel_id=1, source_target_pairs={{0,240},{8,248},{16,0},{24,8},{32,16},{40,24},{48,32},{56,40},{64,... | collective-permute-start | bytes 393224 | tf_op jit(solution)/shard_map/ppermute | solution.py:33
  206.1 6.2 %copy-start.1 = (bf16[15,256,128]{1,2,0:T(8,128)(2,1)S(1)}, bf16[15,256,128]{1,2,0:T(8,128)(2,1)}, u32[]{:S(2)}) copy-start(bf16[15,256,128]{1,2,0:T(8,128)(2,1)} %get-tuple-element.44) | copy-start | bytes 2949124
  209.2 11.2 %collective-permute-start.14 = (f32[256,128]{0,1:T(8,128)}, f32[256,128]{0,1:T(8,128)}, u32[]{:S(2)}, u32[]{:S(2)}) collective-permute-start(f32[256,128]{0,1:T(8,128)} %fusion.85), channel_id=1, source_target_pairs={{0,248},{8,0},{16,8},{24,16},{32,24},{40,32},{48,40},{56,48},{64,5... | collective-permute-start | bytes 393224 | tf_op jit(solution)/shard_map/ppermute | solution.py:33
  216.7 3.7 %collective-permute-start.15 = (f32[256,128]{0,1:T(8,128)}, f32[256,128]{0,1:T(8,128)}, u32[]{:S(2)}, u32[]{:S(2)}) collective-permute-start(f32[256,128]{0,1:T(8,128)} %fusion.97), channel_id=1, source_target_pairs={{0,8},{8,16},{16,24},{24,32},{32,40},{40,48},{48,56},{56,64},{64,7... | collective-permute-start | bytes 393224 | tf_op jit(solution)/shard_map/ppermute | solution.py:33
  219.5 6.7 %collective-permute-start.16 = (f32[256,128]{0,1:T(8,128)S(1)}, f32[256,128]{0,1:T(8,128)S(1)}, u32[]{:S(2)}, u32[]{:S(2)}) collective-permute-start(f32[256,128]{0,1:T(8,128)S(1)} %fusion.109), channel_id=1, source_target_pairs={{0,16},{8,24},{16,32},{24,40},{32,48},{40,56},{48,64},{56,72},{64,... | collective-permute-start | bytes 393224 | tf_op jit(solution)/shard_map/ppermute | solution.py:33
  220.4 5.9 %copy-start.8 = (f32[256,128]{0,1:T(8,128)}, f32[256,128]{0,1:T(8,128)S(1)}, u32[]{:S(2)}) copy-start(f32[256,128]{0,1:T(8,128)S(1)} %collective-permute-done.13) | copy-start | bytes 393220
  228.6 18.8 %copy-start.7 = (bf16[128,256]{1,0:T(8,128)(2,1)S(1)}, bf16[128,256]{1,0:T(8,128)(2,1)}, u32[]{:S(2)}) copy-start(bf16[128,256]{1,0:T(8,128)(2,1)} %get-tuple-element.77) | copy-start | bytes 196612
where the time goes:
time: 250 us; the launch traced here: 248 us
  matrix products  62.5 us (25%)
  blocking collectives  54.9 us (22%)
  starting transfers between devices  46.9 us (19%)
  local copies, waits for them, and re-layouts  41.9 us (17%)
  waiting for transfers between devices  30.2 us (12%)
  other arithmetic  11.5 us (5%)
    dot_general x20, matrix products, contract_rows(): lax.dot_general(block_cols, masked, (((0,), (0,)), ((), ())), preferred_e...  56.5 us
    all_to_all x3, blocking collectives, sent_to_all(): return lax.all_to_all(copies, axis, split_axis=0, concat_axis=0, tiled=True)  54.9 us
    mul x21, local copies, waits for them, and re-layouts, local(): window * active[:, offset][:, None, None]  33.2 us
    ppermute x16, starting transfers between devices, from_behind_2(): lax.ppermute(shard, axis, [(i, (i + by) % devices) for i in range(devices)])  29.2 us
    ppermute x16, waiting for transfers between devices, from_behind_2(): lax.ppermute(shard, axis, [(i, (i + by) % devices) for i in range(devices)])  18.2 us
    all_to_all x1, waiting for transfers between devices, sent_to_all(): return lax.all_to_all(copies, axis, split_axis=0, concat_axis=0, tiled=True)  11.9 us
    all_to_all x1, starting transfers between devices, sent_to_all(): return lax.all_to_all(copies, axis, split_axis=0, concat_axis=0, tiled=True)  8.73 us
    mul x4, other arithmetic, local(): window * active[:, offset][:, None, None]  8.33 us
  transfers between devices with their start and end apart: 19, of which 5 were waited for; matrix products, arithmetic and copies ran while one was open for 30% of the time, Pallas kernels for 0%

commit v1 on v0

v1 whole, which is shorter than its diff:
```python
import functools

import jax
import jax.numpy as jnp
from jax import lax
from jax.experimental import pallas as pl
from jax.experimental.pallas import tpu as pltpu
from jax.sharding import PartitionSpec as P

NEAR = 5
HALF = NEAR // 2
CAP = 16
MESH = pl.DeviceIdType.MESH
F32 = jnp.float32
BF16 = jnp.bfloat16


def remote(src, dst, send, recv, patch, lag):
    return pltpu.make_async_remote_copy(
        src_ref=src,
        dst_ref=dst,
        send_sem=send,
        recv_sem=recv,
        device_id={"patch": patch, "lag": lag},
        device_id_type=MESH,
    )


def dot(a, b):
    return jnp.dot(a, b, preferred_element_type=F32)


def dot_rows(a, b):
    return lax.dot_general(a, b, (((0,), (0,)), ((), ())), preferred_element_type=F32)


def iota(shape, dim):
    return lax.broadcasted_iota(jnp.int32, shape, dim)


def kernel(
    patches, lags, w_hbm, h_hbm, inv_ref, range_ref, tile_ref, panel_ref, resid_ref, out_ref,
    w_buf, h_buf, rim_buf, ht, acc, sbuf, rbuf, nsend, nbuf, src_out, src_in, source, dens, cacc, csend, cbuf,
    w_sem, h_sem, rim_ss, rim_rs, src_ss, src_rs, rs_ss, rs_rs, nb_ss, nb_rs, ag_ss, ag_rs, ch_ss, ch_rs,
):
    t, l = lax.axis_index("patch"), lax.axis_index("lag")
    band, width, cols = w_buf.shape
    steps, shots, _ = sbuf.shape
    chunk = shots // lags
    rim = steps - 1
    is_first = l == 0

    def patch_at(d):
        return lax.rem(t + d + patches, patches)

    def lag_at(d):
        return lax.rem(l + d, lags)

    h_copy = pltpu.make_async_copy(h_hbm, h_buf, h_sem)
    h_copy.start()

    def w_copy(j):
        return pltpu.make_async_copy(w_hbm.at[j], w_buf.at[j], w_sem.at[j])

    for j in [*range(rim, band), *range(rim)]:
        w_copy(j).start()

    barrier = pltpu.get_barrier_semaphore()

    def greet(patch, lag):
        pl.semaphore_signal(barrier, inc=1, device_id={"patch": patch, "lag": lag}, device_id_type=MESH)

    for d in range(1, lags):
        greet(t, lag_at(d))

    def greet_patch(d, carry):
        greet(patch_at(d), l)
        return carry

    lax.fori_loop(1, patches, greet_patch, 0)
    near_by = [d for d in range(-HALF, HALF + 1) if d != 0]

    @pl.when(is_first)
    def _():
        for d in near_by:
            for other in range(1, lags):
                greet(patch_at(d), other)

    @pl.when(l != 0)
    def _():
        for d in near_by:
            greet(patch_at(d), 0)

    recv = tile_ref.shape[1]
    diagonal = iota((recv, recv), 0) == iota((recv, recv), 1)

    def as_column(row):
        return jnp.sum(jnp.where(diagonal, row.astype(F32), 0.0), axis=1, keepdims=True)

    tile_col = as_column(tile_ref[...])
    panel_col = as_column(panel_ref[...])
    named = (tile_col == iota((recv, 128), 1).astype(F32)).astype(F32)
    earlier = (iota((recv, recv), 1) < iota((recv, recv), 0)).astype(BF16)
    rank = jnp.sum(dot(earlier, named.astype(BF16)) * named, axis=1, keepdims=True)
    slot = tile_col * CAP + rank
    placer = (slot == iota((recv, patches * CAP), 1).astype(F32)).astype(BF16)
    src_width = src_out.shape[1]
    mine = jnp.zeros((recv, src_width), F32)
    for s in range(steps):
        lane, place = iota((shots, src_width), 0), iota((shots, src_width), 1)
        pick = (lane - l * chunk == place - s * chunk) & (place >= s * chunk) & (place < (s + 1) * chunk)
        mine = mine + dot(resid_ref[s], pick.astype(BF16))
    mine = jnp.where(iota((recv, src_width), 1) == steps * chunk, panel_col + 1.0, mine).astype(BF16)
    src_out[...] = dot_rows(placer, mine).astype(BF16)
    own_slots = pl.ds(pl.multiple_of(t * CAP, CAP), CAP)
    src_in[own_slots, :] = src_out[own_slots, :]

    h_copy.wait()
    pl.semaphore_wait(barrier, jnp.where(is_first, lags - 1 + patches - 1 + 4 * (lags - 1), lags - 1 + patches - 1 + 4))

    rim_copy = remote(h_buf.at[pl.ds(band - rim, rim)], rim_buf, rim_ss, rim_rs, t, lag_at(1))
    rim_copy.start()

    def slots(p):
        return pl.ds(pl.multiple_of(p * CAP, CAP), CAP)

    def src_copy(d):
        to = patch_at(d)
        return remote(src_out.at[slots(to)], src_in.at[own_slots], src_ss.at[to], src_rs.at[t], to, l)

    def src_start(d, carry):
        src_copy(d).start()
        return carry

    lax.fori_loop(1, patches, src_start, 0)

    def turn(j, carry):
        ht[pl.ds(pl.multiple_of((band - 1 - j) * shots, shots), shots), :] = h_buf[j].T
        return carry

    lax.fori_loop(0, band, turn, 0)
    acc[...] = jnp.zeros_like(acc)

    def is_active(lag_number, i):
        low, high = range_ref[0, i], range_ref[0, NEAR + i]
        return jnp.where((lag_number >= low) & (lag_number < high), 1.0, 0.0).astype(F32)

    def add_lag(j, first_row, rows):
        for i in range(NEAR):
            at = pl.ds(i * width, width)
            left = ht[pl.ds(pl.multiple_of((band - 1 - j) * shots + first_row, shots), rows), :]
            acc[pl.ds(first_row, rows), at] += is_active(l * band + j + 1, i) * dot(left, w_buf[j, :, at])

    def later_lag(j, carry):
        w_copy(j).wait()
        add_lag(j, 0, steps * shots)
        return carry

    def early_lag(j, carry):
        w_copy(j).wait()
        add_lag(j, 0, shots)
        return carry

    def early_lag_rest(j, carry):
        add_lag(j, shots, (steps - 1) * shots)
        return carry

    lax.fori_loop(rim, band, later_lag, 0)
    lax.fori_loop(0, rim, early_lag, 0)

    def rs_copy(s, d):
        to = lag_at(d)
        part = pl.ds(pl.multiple_of(to * chunk, chunk), chunk)
        return remote(sbuf.at[s, part], rbuf.at[s, l], rs_ss.at[s, to], rs_rs.at[s, l], t, to)

    def send_step(s):
        sbuf[s] = acc[pl.ds(s * shots, shots), :].astype(BF16)
        for d in range(1, lags):
            rs_copy(s, d).start()

    send_step(0)
    rim_copy.wait()
    for q in range(rim):
        before = rim_buf[q]
        ht[pl.ds((band + rim - 1 - q) * shots, shots), :] = jnp.where(is_first, jnp.zeros_like(before.T), before.T)
    lax.fori_loop(0, rim, early_lag_rest, 0)
    for s in range(1, steps):
        send_step(s)

    def src_wait(d, carry):
        of = patch_at(d)
        remote(src_in.at[slots(of)], src_in.at[slots(of)], src_ss.at[of], src_rs.at[of], of, l).wait_recv()
        return carry

    lax.fori_loop(1, patches, src_wait, 0)
    labels = src_in[:, pl.ds(steps * chunk, 1)].astype(F32)
    onto = (labels == (iota((patches * CAP, width), 1) + 1).astype(F32)).astype(BF16)
    source[...] = dot_rows(src_in[...], onto)

    own_shots = pl.ds(pl.multiple_of(l * chunk, chunk), chunk)

    def nb_copy(s, i):
        return remote(nsend.at[s, i], nbuf.at[s, i], nb_ss.at[s, i], nb_rs.at[s, i], patch_at(i - HALF), l)

    def ag_copy(s, d):
        to = lag_at(d)
        return remote(dens.at[s, own_shots], dens.at[s, own_shots], ag_ss.at[s, to], ag_rs.at[s, l], t, to)

    def ag_wait(s):
        for d in range(1, lags):
            of = lag_at(d)
            part = pl.ds(pl.multiple_of(of * chunk, chunk), chunk)
            remote(dens.at[s, part], dens.at[s, part], ag_ss.at[s, of], ag_rs.at[s, of], t, of).wait_recv()

    def ch_copy(n, i, lag):
        return remote(
            csend.at[n - 1, pl.ds(lag * chunk, chunk), pl.ds(i * width, width)],
            cbuf.at[n - 1, i], ch_ss.at[n - 1, i * lags + lag], ch_rs.at[n - 1, i], patch_at(i - HALF), lag,
        )

    def new_terms(k, s, i):
        return is_active(k, i) * dot(dens[s], w_buf[k - 1, :, pl.ds(i * width, width)])

    for s in range(steps):
        if s > 0:
            @pl.when(is_first)
            def _():
                ag_wait(s - 1)
                for i in range(NEAR):
                    at = pl.ds(i * width, width)
                    value = new_terms(1, s - 1, i)
                    if s > 1:
                        value = value + cacc[s - 2, :, at]
                    csend[s - 1, :, at] = value.astype(BF16)
                    for lag in range(lags):
                        if i == HALF and lag == 0:
                            cbuf[s - 1, i] = value[:chunk].astype(BF16)
                        else:
                            ch_copy(s, i, lag).start()

        total = acc[pl.ds(pl.multiple_of(s * shots + l * chunk, chunk), chunk), :]
        for d in range(1, lags):
            of = lag_at(d)
            remote(rbuf.at[s, of], rbuf.at[s, of], rs_ss.at[s, of], rs_rs.at[s, of], t, of).wait_recv()
            total = total + rbuf[s, of].astype(F32)
        for i in range(NEAR):
            if i == HALF:
                nbuf[s, i] = total[:, i * width : (i + 1) * width]
            else:
                nsend[s, i] = total[:, i * width : (i + 1) * width]
                nb_copy(s, i).start()
        if 0 < s < steps - 1:
            @pl.when(is_first)
            def _():
                for n in range(s + 1, steps):
                    k = n - s + 1
                    for i in range(NEAR):
                        at = pl.ds(i * width, width)
                        value = new_terms(k, s - 1, i)
                        if s > 1:
                            value = value + cacc[n - 2, :, at]
                        cacc[n - 2, :, at] = value
        incoming = nbuf[s, HALF]
        for i in range(NEAR):
            if i != HALF:
                remote(nbuf.at[s, i], nbuf.at[s, i], nb_ss.at[s, i], nb_rs.at[s, i], patch_at(HALF - i), l).wait_recv()
                incoming = incoming + nbuf[s, i]
        if s > 0:
            for i in range(NEAR):
                arrival = remote(cbuf.at[s - 1, i], cbuf.at[s - 1, i], ch_ss.at[s - 1, 0], ch_rs.at[s - 1, i], patch_at(HALF - i), 0)
                if i != HALF:
                    arrival.wait_recv()
                else:
                    pl.when(l != 0)(arrival.wait_recv)
                incoming = incoming + cbuf[s - 1, i].astype(F32)
        right = (source[pl.ds(s * chunk, chunk), :] - incoming).astype(BF16)
        dens[s, own_shots, :] = dot(right, inv_ref[...]).astype(BF16)
        for d in range(1, lags):
            ag_copy(s, d).start()

    for s in range(steps):
        if s < steps - 1:
            @pl.when(l != 0)
            def _():
                ag_wait(s)
        else:
            ag_wait(s)
    out_ref[...] = dens[...]

    def src_sent(d, carry):
        src_copy(d).wait_send()
        return carry

    lax.fori_loop(1, patches, src_sent, 0)
    for s in range(steps):
        for d in range(1, lags):
            rs_copy(s, d).wait_send()
            ag_copy(s, d).wait_send()
        for i in range(NEAR):
            if i != HALF:
                nb_copy(s, i).wait_send()

    @pl.when(is_first)
    def _():
        for n in range(1, steps):
            for i in range(NEAR):
                for lag in range(lags):
                    if not (i == HALF and lag == 0):
                        ch_copy(n, i, lag).wait_send()


def local(patches, lags, interaction, history, near_inverse, lag_ranges, receiver_tile, receiver_panel, residuals):
    band, width, cols = interaction.shape
    shots = history.shape[2]
    recv, steps, _ = residuals.shape
    chunk = shots // lags
    src_width = -(-(steps * chunk + 1) // 128) * 128
    any_space = pl.BlockSpec(memory_space=pl.ANY)
    vmem = pl.BlockSpec(memory_space=pltpu.VMEM)
    dma = pltpu.SemaphoreType.DMA
    out = pl.pallas_call(
        functools.partial(kernel, patches, lags),
        out_shape=jax.ShapeDtypeStruct((steps, shots, width), BF16),
        in_specs=[any_space, any_space, vmem, pl.BlockSpec(memory_space=pltpu.SMEM), vmem, vmem, vmem],
        out_specs=vmem,
        scratch_shapes=[
            pltpu.VMEM((band, width, cols), BF16),
            pltpu.VMEM((band, width, shots), BF16),
            pltpu.VMEM((steps - 1, width, shots), BF16),
            pltpu.VMEM(((band + steps - 1) * shots, width), BF16),
            pltpu.VMEM((steps * shots, cols), F32),
            pltpu.VMEM((steps, shots, cols), BF16),
            pltpu.VMEM((steps, lags, chunk, cols), BF16),
            pltpu.VMEM((steps, NEAR, chunk, width), F32),
            pltpu.VMEM((steps, NEAR, chunk, width), F32),
            pltpu.VMEM((patches * CAP, src_width), BF16),
            pltpu.VMEM((patches * CAP, src_width), BF16),
            pltpu.VMEM((src_width, width), F32),
            pltpu.VMEM((steps, shots, width), BF16),
            pltpu.VMEM((steps - 2, shots, cols), F32),
            pltpu.VMEM((steps - 1, shots, cols), BF16),
            pltpu.VMEM((steps - 1, NEAR, chunk, width), BF16),
            dma((band,)), dma, dma, dma, dma((patches,)), dma((patches,)),
            dma((steps, lags)), dma((steps, lags)), dma((steps, NEAR)), dma((steps, NEAR)),
            dma((steps, lags)), dma((steps, lags)), dma((steps - 1, NEAR * lags)), dma((steps - 1, NEAR)),
        ],
        compiler_params=pltpu.CompilerParams(collective_id=0, has_side_effects=True, vmem_limit_bytes=60 * 1024 * 1024),
        name="march",
    )(
        interaction, history, near_inverse, lag_ranges, receiver_tile.reshape(1, recv), receiver_panel.reshape(1, recv),
        jnp.swapaxes(residuals, 0, 1),
    )
    return jnp.swapaxes(out, 1, 2)


def solution(mesh):
    in_specs = (
        P("lag", "patch", None),
        P("lag", "patch", None),
        P("patch", None),
        P("patch", None),
        P("patch", None),
        P("patch"),
        P("patch", None, None),
    )
    body = functools.partial(local, mesh.shape["patch"], mesh.shape["lag"])
    return jax.shard_map(body, mesh=mesh, in_specs=in_specs, out_specs=P(None, "patch", None), check_vma=False)
```

time: 250 us -> 85.3 us (0.34)
  Pallas kernels: 0 us -> 81.7 us
  matrix products: 62.5 us -> 0 us
  blocking collectives: 54.9 us -> 0 us
  starting transfers between devices: 46.9 us -> 0 us
  local copies, waits for them, and re-layouts: 41.9 us -> 3.48 us
  waiting for transfers between devices: 30.2 us -> 0 us
  other arithmetic: 11.5 us -> 0 us
    pallas_call x0 -> x1, Pallas kernels: none -> 81.7 us  [local(): pl.pallas_call(functools.partial(kernel, patches, lags), out_shape=jax.Sh...]
    dot_general x27 -> x0, matrix products: 62.5 us -> none  [the longest x20 56.5 us: contract_rows(): lax.dot_general(block_cols, masked, (((0,), (0,)), ((), ())), preferred_e...]
    all_to_all x3 -> x0, blocking collectives: 54.9 us -> none  [sent_to_all(): return lax.all_to_all(copies, axis, split_axis=0, concat_axis=0, tiled=True)]
    ppermute x17 -> x0, starting transfers between devices: 33.7 us -> none  [the longest x16 29.2 us: from_behind_2(): lax.ppermute(shard, axis, [(i, (i + by) % devices) for i in range(devices)])]
    mul x21 -> x0, local copies, waits for them, and re-layouts: 33.2 us -> none  [local(): window * active[:, offset][:, None, None]]
    ppermute x17 -> x0, waiting for transfers between devices: 18.2 us -> none  [the longest x16 18.2 us: from_behind_2(): lax.ppermute(shard, axis, [(i, (i + by) % devices) for i in range(devices)])]
    all_to_all x2 -> x0, starting transfers between devices: 13.1 us -> none  [the longest x1 8.73 us: sent_to_all(): return lax.all_to_all(copies, axis, split_axis=0, concat_axis=0, tiled=True)]
    all_to_all x2 -> x0, waiting for transfers between devices: 11.9 us -> none  [the longest x1 11.9 us: sent_to_all(): return lax.all_to_all(copies, axis, split_axis=0, concat_axis=0, tiled=True)]
  transfers between devices with their start and end apart: 19 -> 0, of which waited for: 5 -> 0; matrix products, arithmetic and copies ran while one was open for 30% -> 0% of each run, Pallas kernels for 0% -> 0%
where the time goes in v1:
time: 85.3 us; the launch traced here: 85.2 us
  Pallas kernels  81.7 us (96%)
  local copies, waits for them, and re-layouts  3.48 us (4%)
    pallas_call x1, Pallas kernels, local(): pl.pallas_call(functools.partial(kernel, patches, lags), out_shape=jax.Sh...  81.7 us
    transpose x1, local copies, waits for them, and re-layouts, local(): return jnp.swapaxes(out, 1, 2)  1.79 us

profile of v1, /device:TPU:1, one launch (start us, length us, event | category | flops | bytes accessed | tf_op | source)
XLA Modules:
  0.0 85.2 jit_solution(10498899414088450113)
XLA Ops:
  0.0 1.7 %copy.11 = bf16[256,4,128]{2,0,1:T(8,128)(2,1)} copy(bf16[256,4,128]{2,1,0:T(4,128)(2,1)} %param.13) | data formatting | bytes 524288 | tf_op args[6]
  1.7 81.7 %march.1 = bf16[4,128,256]{2,1,0:T(8,128)(2,1)} custom-call(bf16[15,256,1280]{2,1,0:T(8,128)(2,1)} %w_hbm.1, bf16[15,256,128]{2,1,0:T(8,128)(2,1)} %h_hbm.1, bf16[256,256]{1,0:T(8,128)(2,1)} %inv_ref.1, s32[1,10]{1,0:T(1,128)} %range_ref.1, s32[1,256]{1,0:T(1,128)} %bitcast.8, s32[1,256]{1,0:T(1,128)} %bitcast.9, bf16[4,256,128]{2,1,0:T(8,128)(2,1)} %bitcast.7), custom_call_target="tpu_custom_call" | custom-call | tf_op jit(solution)/shard_map/march/pallas_call | solution.py:321
  83.4 1.8 %copy.9 = bf16[4,256,128]{2,1,0:T(8,128)(2,1)} copy(bf16[4,256,128]{1,2,0:T(8,128)(2,1)} %bitcast.6) | data formatting | bytes 524288 | tf_op jit(solution)/shard_map/transpose | solution.py:353

commit v2 on v1

v2 whole, which is shorter than its diff:
```python
import functools

import jax
import jax.numpy as jnp
from jax import lax
from jax.experimental import pallas as pl
from jax.experimental.pallas import tpu as pltpu
from jax.sharding import PartitionSpec as P

NEAR = 5
HALF = NEAR // 2
CAP = 16
GROUPS = 2
MESH = pl.DeviceIdType.MESH
F32 = jnp.float32
BF16 = jnp.bfloat16


def remote(src, dst, send, recv, patch, lag):
    return pltpu.make_async_remote_copy(
        src_ref=src,
        dst_ref=dst,
        send_sem=send,
        recv_sem=recv,
        device_id={"patch": patch, "lag": lag},
        device_id_type=MESH,
    )


def landed(region, sem):
    pltpu.make_async_copy(region, region, sem).wait()


def dot(a, b):
    return jnp.dot(a, b, preferred_element_type=F32)


def dot_rows(a, b):
    return lax.dot_general(a, b, (((0,), (0,)), ((), ())), preferred_element_type=F32)


def iota(shape, dim):
    return lax.broadcasted_iota(jnp.int32, shape, dim)


def kernel(
    patches, lags, w_hbm, h_hbm, inv_hbm, range_ref, tile_ref, panel_ref, resid_hbm, out_ref,
    w_buf, h_buf, inv_ref, resid_ref, rim_buf, ht, acc, got, sbuf, rbuf, psend, own_send, pbuf, nsend, nbuf, own_last, src_out, src_in, source, dens, cacc, csend, cgot, cbuf,
    w_sem, h_sem, inv_sem, resid_sem, rim_ss, rim_rs, src_ss, src_rs, rs_ss, rs_rs, p_ss, p_rs, nb_ss, nb_rs,
    ag_ss, ag_rs, pass_ss, pair_ss, pair_rs, ch_ss, ch_rs, out_ss, out_rs, sp_ss, sp_rs,
):
    t, l = lax.axis_index("patch"), lax.axis_index("lag")
    band, width, cols = w_buf.shape
    core = lax.rem(t, 2)
    given, kept = HALF * width, (HALF + 1) * width
    steps, shots, _ = sbuf.shape
    chunk = shots // lags
    rim = steps - 1
    groups = GROUPS
    group = shots // groups
    is_first = l == 0

    def patch_at(d):
        return lax.rem(t + d + patches, patches)

    def lag_at(d):
        return lax.rem(l + d, lags)

    resid_copy = pltpu.make_async_copy(resid_hbm, resid_ref, resid_sem)
    resid_copy.start()
    h_copy = pltpu.make_async_copy(h_hbm, h_buf, h_sem)
    h_copy.start()
    inv_copy = pltpu.make_async_copy(inv_hbm, inv_ref, inv_sem)

    per = band // w_sem.shape[0]

    def w_copy(a):
        lags_of = pl.ds(a * per, per)
        return pltpu.make_async_copy(w_hbm.at[lags_of], w_buf.at[lags_of], w_sem.at[a])

    w_copy(0).start()

    barrier = pltpu.get_barrier_semaphore()

    def greet(patch, lag):
        pl.semaphore_signal(barrier, inc=1, device_id={"patch": patch, "lag": lag}, device_id_type=MESH)

    for d in range(1, lags):
        greet(t, lag_at(d))

    def greet_patch(d, carry):
        greet(patch_at(d), l)
        return carry

    lax.fori_loop(1, patches, greet_patch, 0)
    near_by = [d for d in range(-HALF, HALF + 1) if d != 0]

    @pl.when(is_first)
    def _():
        for d in near_by:
            for other in range(1, lags):
                greet(patch_at(d), other)

    @pl.when(l != 0)
    def _():
        for d in near_by:
            greet(patch_at(d), 0)

    def turn(j, carry):
        ht[pl.ds(pl.multiple_of((band - 1 - j) * shots, shots), shots), :] = h_buf[j].T
        return carry

    with jax.named_scope("turn"):
        h_copy.wait()
        for a in range(1, band // per):
            w_copy(a).start()
        inv_copy.start()
        lax.fori_loop(0, band, turn, 0)

    def is_active(lag_number, i):
        low, high = range_ref[0, i], range_ref[0, NEAR + i]
        return jnp.where((lag_number >= low) & (lag_number < high), 1.0, 0.0).astype(F32)

    def patch_block(q):
        return q + (HALF + 1) * (1 - core) if q < HALF else q - HALF + HALF * core

    def lag_terms(j, q, first_row, rows):
        i = patch_block(q)
        left = ht[pl.ds(pl.multiple_of((band - 1 - j) * shots + first_row, shots), rows), :]
        right = w_buf[j, :, pl.ds(pl.multiple_of(i * width, width), width)]
        return is_active(l * band + j + 1, i) * dot(left, right)

    def add_lag(j, first_row, rows):
        for q in range(NEAR):
            acc[pl.ds(first_row, rows), pl.ds(q * width, width)] += lag_terms(j, q, first_row, rows)

    def set_lag(j, first_row, rows):
        for q in range(NEAR):
            acc[pl.ds(first_row, rows), pl.ds(q * width, width)] = lag_terms(j, q, first_row, rows)

    def pair_copy(first, count, at):
        rows = pl.ds(first * shots, count * shots)
        return remote(acc.at[rows, pl.ds(0, given)], got.at[rows], pair_ss, pair_rs.at[at], t + 1 - 2 * core, l)

    def pair_wait(first, count):
        landed(got.at[pl.ds(first * shots, count * shots)], pair_rs.at[min(first, 2)])

    def first_step(j, carry):
        add_lag(j, 0, shots)
        return carry

    def later_steps(j, carry):
        add_lag(j, shots, (steps - 1) * shots)
        return carry

    def second_step_rim(j, carry):
        add_lag(j, shots, shots)
        return carry

    def last_steps_rim(j, carry):
        add_lag(j, 2 * shots, (steps - 2) * shots)
        return carry

    def rim_copy(first, count, at):
        return remote(h_buf.at[pl.ds(band - rim + first, count)], rim_buf.at[pl.ds(first, count)], rim_ss.at[at], rim_rs.at[at], t, lag_at(1))

    def turn_rim(q):
        before = rim_buf[q].T
        ht[pl.ds((band + rim - 1 - q) * shots, shots), :] = jnp.where(is_first, jnp.zeros_like(before), before)

    def slots(p):
        return pl.ds(pl.multiple_of(p * CAP, CAP), CAP)

    own_slots = pl.ds(pl.multiple_of(t * CAP, CAP), CAP)

    def src_copy(d):
        to = patch_at(d)
        return remote(src_out.at[slots(to)], src_in.at[own_slots], src_ss, src_rs, to, l)

    def src_start(d, carry):
        src_copy(d).start()
        return carry

    def rs_copy(s, d):
        to = lag_at(d)
        part = pl.ds(pl.multiple_of(to * chunk, chunk), chunk)
        return remote(sbuf.at[s, part], rbuf.at[s, l], rs_ss, rs_rs.at[s], t, to)

    def send_step(s):
        rows = pl.ds(s * shots, shots)
        shared = pl.ds(pl.multiple_of(given + width * (1 - core), width), given)
        acc[rows, shared] += got[rows, :]
        sbuf[s] = acc[rows, pl.ds(given, kept)].astype(BF16)
        for d in range(1, lags):
            rs_copy(s, d).start()

    own_shots = pl.ds(pl.multiple_of(l * chunk, chunk), chunk)

    last = steps - 1

    def lag_sum(s):
        total = acc[pl.ds(pl.multiple_of(s * shots + l * chunk, chunk), chunk), pl.ds(given, kept)]
        landed(rbuf.at[s, pl.ds(0, lags - 1)], rs_rs.at[s])
        for d in range(1, lags):
            total = total + rbuf[s, lag_at(d)].astype(F32)
        parts = [total[:, m * width : (m + 1) * width] for m in range(HALF + 1)]
        own = jnp.where(core == 0, parts[HALF], parts[0]) - source[pl.ds(s * chunk, chunk), :]
        return parts, own

    def owner(f):
        return patch_at(f - HALF + (HALF + 1) * core)

    def piece_rows(side, lag):
        return pl.ds(pl.multiple_of(side * shots + lag * chunk, chunk), chunk)

    def piece_copy(s, f):
        return remote(psend.at[s, f + core], pbuf.at[s, piece_rows(HALF - core, l)], p_ss, p_rs.at[s], owner(f), 0)

    def own_piece_copy(s):
        return remote(own_send.at[s], pbuf.at[s, piece_rows(0, l)], p_ss, p_rs.at[s], t, 0)

    def pieces(s):
        parts, own = lag_sum(s)
        for m in range(HALF + 1):
            psend[s, m] = parts[m].astype(BF16)
        for f in range(HALF):
            piece_copy(s, f).start()

        @pl.when(is_first)
        def _():
            pbuf[s, pl.ds(0, chunk), :] = own.astype(BF16)

        @pl.when(l != 0)
        def _():
            own_send[s] = own.astype(BF16)
            own_piece_copy(s).start()

    def piece_wait(s):
        landed(pbuf.at[s, pl.ds(chunk, (HALF + 1) * shots - chunk)], p_rs.at[s])

    def piece_sum(s, first, count):
        sides = [pbuf[s, pl.ds(side * shots + first, count), :].astype(F32) for side in range(HALF + 1)]
        return sides[0] + sides[1] + sides[2]

    def nb_copy(f):
        return remote(nsend.at[f + core], nbuf.at[1 - core], nb_ss, nb_rs, owner(f), l)

    def last_sum():
        parts, own = lag_sum(last)
        for m in range(HALF + 1):
            nsend[m] = parts[m]
        for f in range(HALF):
            nb_copy(f).start()
        return own

    def nb_sum(own):
        landed(nbuf, nb_rs)
        return own + nbuf[0] + nbuf[1]

    def density_of(right):
        return dot(right.astype(BF16), inv_ref[...]).astype(BF16)

    def ag_copy(s, d, sent):
        return remote(dens.at[s, own_shots], dens.at[s, own_shots], sent, ag_rs, t, lag_at(d))

    with jax.named_scope("first"):
        w_copy(0).wait()
        set_lag(0, 0, shots)
        lax.fori_loop(1, per, first_step, 0)
        for a in range(1, band // per):
            w_copy(a).wait()
            lax.fori_loop(a * per, (a + 1) * per, first_step, 0)
    with jax.named_scope("bar"):
        pl.semaphore_wait(barrier, jnp.where(is_first, lags - 1 + patches - 1 + 4 * (lags - 1), lags - 1 + patches - 1 + 4))
    with jax.named_scope("pair0"):
        pair_copy(0, 1, 0).start()
        rim_copy(rim - 1, 1, 0).start()

    with jax.named_scope("prep"):
        recv = tile_ref.shape[1]
        diagonal = iota((recv, recv), 0) == iota((recv, recv), 1)

        def as_column(row):
            return jnp.sum(jnp.where(diagonal, row.astype(F32), 0.0), axis=1, keepdims=True)

        tile_col = as_column(tile_ref[...])
        panel_col = as_column(panel_ref[...])
        named = (tile_col == iota((recv, 128), 1).astype(F32)).astype(F32)
        earlier = (iota((recv, recv), 1) < iota((recv, recv), 0)).astype(BF16)
        rank = jnp.sum(dot(earlier, named.astype(BF16)) * named, axis=1, keepdims=True)
        slot = tile_col * CAP + rank
        placer = (slot == iota((recv, patches * CAP), 1).astype(F32)).astype(BF16)
        src_width = src_out.shape[1]
        mine = jnp.zeros((recv, src_width), F32)
        resid_copy.wait()
        for s in range(steps):
            lane, place = iota((shots, src_width), 0), iota((shots, src_width), 1)
            pick = (lane - l * chunk == place - s * chunk) & (place >= s * chunk) & (place < (s + 1) * chunk)
            mine = mine + dot(resid_ref[:, s, :], pick.astype(BF16))
        mine = jnp.where(iota((recv, src_width), 1) == steps * chunk, panel_col + 1.0, mine).astype(BF16)
        src_out[...] = dot_rows(placer, mine).astype(BF16)
        src_in[own_slots, :] = src_out[own_slots, :]

    with jax.named_scope("src0"):
        lax.fori_loop(1, patches, src_start, 0)
    with jax.named_scope("pairwait0"):
        pair_wait(0, 1)
    with jax.named_scope("send0"):
        send_step(0)
        rim_copy(0, rim - 1, 1).start()
    with jax.named_scope("later2"):
        set_lag(rim, shots, (steps - 1) * shots)
        lax.fori_loop(rim + 1, band, later_steps, 0)

    with jax.named_scope("rim1"):
        rim_copy(rim - 1, 1, 0).wait()
        turn_rim(rim - 1)
        lax.fori_loop(0, rim, second_step_rim, 0)
        pair_copy(1, 1, 1).start()

    with jax.named_scope("srcwait"):
        landed(src_in.at[pl.ds(0, (patches - 1) * CAP)], src_rs)
        inv_copy.wait()
    with jax.named_scope("src"):
        labels = src_in[:, pl.ds(steps * chunk, 1)].astype(F32)
        onto = (labels == (iota((patches * CAP, width), 1) + 1).astype(F32)).astype(BF16)
        source[...] = dot_rows(src_in[...], onto)

    with jax.named_scope("send1"):
        pair_wait(1, 1)
        send_step(1)
    with jax.named_scope("rs0"):
        pieces(0)
    with jax.named_scope("rimwait"):
        rim_copy(0, rim - 1, 1).wait()
    with jax.named_scope("rim23"):
        for q in range(rim - 1):
            turn_rim(q)
        lax.fori_loop(0, rim, last_steps_rim, 0)
        pair_copy(2, steps - 2, 2).start()
    with jax.named_scope("send23"):
        pair_wait(2, steps - 2)
        for s in range(2, steps):
            send_step(s)
    with jax.named_scope("rs1"):
        pieces(1)

    def place_of(i):
        return HALF * 2 if i == HALF else i - (i > HALF)

    def terms_rows(i, first, count):
        return pl.ds(i * shots + first, count)

    def ch_copy(n, i, g):
        return remote(csend.at[n - 1, terms_rows(i, g * group, group)], cgot.at[n - 1, g, place_of(i)], ch_ss, ch_rs.at[n - 1, g], patch_at(i - HALF), 0)

    def out_copy(i, lag):
        return remote(csend.at[last - 1, terms_rows(i, lag * chunk, chunk)], cbuf.at[place_of(i)], out_ss, out_rs, patch_at(i - HALF), lag)

    def spread_copy(s, part, lag):
        rows = pl.ds(part * chunk, chunk)
        return remote(dens.at[s, rows], dens.at[s, rows], sp_ss, ag_rs if part == 0 else sp_rs.at[s], t, lag)

    def others(d):
        return pl.when(lag_at(d) != 0)

    def new_terms(k, s, i, rows):
        return is_active(k, i) * dot(dens[s, rows, :], w_buf[k - 1, :, pl.ds(i * width, width)])

    def send_terms(n, g):
        rows = pl.ds(g * group, group)
        for i in (0, NEAR - 1, 1, NEAR - 2, *range(2, NEAR - 2)):
            value = new_terms(1, n - 1, i, rows)
            if n > 1:
                value = value + cacc[n - 2, i, rows, :]
            csend[n - 1, terms_rows(i, g * group, group), :] = value.astype(BF16)
            if n < last:
                if i != HALF:
                    ch_copy(n, i, g).start()
            else:
                for lag in range(g * group // chunk, (g + 1) * group // chunk):
                    if i == HALF and lag == 0:
                        cbuf[place_of(i)] = value[:chunk].astype(BF16)
                    else:
                        out_copy(i, lag).start()

    def older_terms(s):
        for n in range(s + 2, steps):
            for i in range(NEAR):
                value = new_terms(n - s, s, i, pl.ds(0, shots))
                if s > 0:
                    value = value + cacc[n - 2, i]
                cacc[n - 2, i] = value

    def finish(n, g):
        rest = -piece_sum(n, g * group, group) - csend[n - 1, terms_rows(HALF, g * group, group), :].astype(F32)
        landed(cgot.at[n - 1, g], ch_rs.at[n - 1, g])
        for i in range(NEAR - 1):
            rest = rest - cgot[n - 1, g, i].astype(F32)
        dens[n, pl.ds(g * group, group), :] = density_of(rest)

    def spread(s):
        for lag in range(1, lags):
            spread_copy(s, lag, lag).start()
            spread_copy(s, 0, lag).start()

    @pl.when(is_first)
    def _():
        with jax.named_scope("p0"):
            piece_wait(0)
        with jax.named_scope("terms1"):
            dens[0] = density_of(-piece_sum(0, 0, shots))
            for g in range(groups):
                send_terms(1, g)
            spread(0)
        with jax.named_scope("older1"):
            older_terms(0)
        with jax.named_scope("rs2"):
            pieces(2)
        with jax.named_scope("rs3"):
            own_last[...] = last_sum()
        for n in range(1, last):
            with jax.named_scope(f"p{n}"):
                piece_wait(n)
            for g in range(groups):
                with jax.named_scope(f"finish{n}{g}"):
                    finish(n, g)
                with jax.named_scope(f"terms{n + 1}{g}"):
                    send_terms(n + 1, g)
            spread(n)
            with jax.named_scope(f"older{n + 1}"):
                older_terms(n)

    @pl.when(l != 0)
    def _():
        with jax.named_scope("rs2"):
            pieces(2)
        with jax.named_scope("rs3"):
            own_last[...] = last_sum()
        with jax.named_scope("sp"):
            for n in range(last):
                landed(dens.at[n, own_shots], sp_rs.at[n])
                for d in range(1, lags):
                    others(d)(ag_copy(n, d, pass_ss).start)

    with jax.named_scope("nblast"):
        rest = -nb_sum(own_last[...])
    with jax.named_scope("outwait"):
        @pl.when(is_first)
        def _():
            landed(cbuf.at[pl.ds(0, NEAR - 1)], out_rs)

        @pl.when(l != 0)
        def _():
            landed(cbuf, out_rs)

        for i in range(NEAR):
            rest = rest - cbuf[i].astype(F32)
    with jax.named_scope("dlast"):
        dens[last, own_shots, :] = density_of(rest)
        for d in range(1, lags):
            ag_copy(last, d, ag_ss).start()

    with jax.named_scope("aglast"):
        seven = pl.ds(0, (lags - 1) * chunk)

        @pl.when(is_first)
        def _():
            landed(dens.at[0, seven], ag_rs)

        @pl.when(l != 0)
        def _():
            landed(dens.at[:, seven], ag_rs)

    with jax.named_scope("fin"):
        for s in range(steps):
            out_ref[s] = dens[s].T
        landed(src_in.at[pl.ds(0, (patches - 1) * CAP)], src_ss)
        landed(rbuf.at[:, pl.ds(0, lags - 1)], rs_ss)
        landed(got, pair_ss)
        landed(nbuf, nb_ss)
        landed(dens.at[0, seven], ag_ss)

        @pl.when(is_first)
        def _():
            landed(pbuf.at[:, pl.ds(0, HALF * chunk)], p_ss)
            landed(cgot, ch_ss)
            landed(csend.at[last - 1, pl.ds(0, (NEAR * lags - 1) * chunk)], out_ss)
            landed(pbuf.at[:, pl.ds(0, 2 * (lags - 1) * chunk)], sp_ss)

        @pl.when(l != 0)
        def _():
            landed(pbuf.at[:, pl.ds(0, (HALF + 1) * chunk)], p_ss)
            landed(dens.at[pl.ds(0, last), pl.ds(0, (lags - 2) * chunk)], pass_ss)


def local(patches, lags, interaction, history, near_inverse, lag_ranges, receiver_tile, receiver_panel, residuals):
    band, width, cols = interaction.shape
    shots = history.shape[2]
    recv, steps, _ = residuals.shape
    chunk = shots // lags
    src_width = -(-(steps * chunk + 1) // 128) * 128
    per = 3 if band % 3 == 0 else 1
    any_space = pl.BlockSpec(memory_space=pl.ANY)
    vmem = pl.BlockSpec(memory_space=pltpu.VMEM)
    dma = pltpu.SemaphoreType.DMA
    out = pl.pallas_call(
        functools.partial(kernel, patches, lags),
        out_shape=jax.ShapeDtypeStruct((steps, width, shots), BF16),
        in_specs=[any_space, any_space, any_space, pl.BlockSpec(memory_space=pltpu.SMEM), vmem, vmem, any_space],
        out_specs=vmem,
        scratch_shapes=[
            pltpu.VMEM((band, width, cols), BF16),
            pltpu.VMEM((band, width, shots), BF16),
            pltpu.VMEM(near_inverse.shape, BF16),
            pltpu.VMEM((recv, steps, shots), BF16),
            pltpu.VMEM((steps - 1, width, shots), BF16),
            pltpu.VMEM(((band + steps - 1) * shots, width), BF16),
            pltpu.VMEM((steps * shots, cols), F32),
            pltpu.VMEM((steps * shots, HALF * width), F32),
            pltpu.VMEM((steps, shots, (HALF + 1) * width), BF16),
            pltpu.VMEM((steps, lags, chunk, (HALF + 1) * width), BF16),
            pltpu.VMEM((steps - 1, HALF + 1, chunk, width), BF16),
            pltpu.VMEM((steps - 1, chunk, width), BF16),
            pltpu.VMEM((steps - 1, (HALF + 1) * shots, width), BF16),
            pltpu.VMEM((HALF + 1, chunk, width), F32),
            pltpu.VMEM((2, chunk, width), F32),
            pltpu.VMEM((chunk, width), F32),
            pltpu.VMEM((patches * CAP, src_width), BF16),
            pltpu.VMEM((patches * CAP, src_width), BF16),
            pltpu.VMEM((src_width, width), F32),
            pltpu.VMEM((steps, shots, width), BF16),
            pltpu.VMEM((steps - 2, NEAR, shots, width), F32),
            pltpu.VMEM((steps - 1, NEAR * shots, width), BF16),
            pltpu.VMEM((steps - 2, GROUPS, NEAR - 1, shots // GROUPS, width), BF16),
            pltpu.VMEM((NEAR, chunk, width), BF16),
            dma((band // per,)), dma, dma, dma, dma((2,)), dma((2,)), dma, dma, dma, dma((steps,)), dma, dma((steps - 1,)), dma, dma,
            dma, dma, dma, dma, dma((3,)), dma, dma((steps - 2, GROUPS)), dma, dma, dma, dma((steps - 1,)),
        ],
        compiler_params=pltpu.CompilerParams(collective_id=0, has_side_effects=True, vmem_limit_bytes=60 * 1024 * 1024),
        name="march",
    )(
        interaction, history, near_inverse, lag_ranges, receiver_tile.reshape(1, recv), receiver_panel.reshape(1, recv),
        residuals,
    )
    return out


def solution(mesh):
    in_specs = (
        P("lag", "patch", None),
        P("lag", "patch", None),
        P("patch", None),
        P("patch", None),
        P("patch", None),
        P("patch"),
        P("patch", None, None),
    )
    body = functools.partial(local, mesh.shape["patch"], mesh.shape["lag"])
    return jax.shard_map(body, mesh=mesh, in_specs=in_specs, out_specs=P(None, "patch", None), check_vma=False)
```

time: 85.3 us -> 62.4 us (0.73)
  Pallas kernels: 81.7 us -> 60.6 us
  local copies, waits for them, and re-layouts: 3.48 us -> 1.67 us
    pallas_call x1, Pallas kernels: 81.7 us -> 60.6 us  [local(): pl.pallas_call(functools.partial(kernel, patches, lags), out_shape=jax.Sh...]
    transpose x1 -> x0, local copies, waits for them, and re-layouts: 1.79 us -> none  [local(): return jnp.swapaxes(out, 1, 2)]
where the time goes in v2:
time: 62.4 us; the launch traced here: 62.3 us
  Pallas kernels  60.6 us (97%)
  local copies, waits for them, and re-layouts  1.67 us (3%)
    pallas_call x1, Pallas kernels, local(): pl.pallas_call(functools.partial(kernel, patches, lags), out_shape=jax.Sh...  60.6 us
    unnamed x1, local copies, waits for them, and re-layouts  1.67 us

profile of v2, /device:TPU:1, one launch (start us, length us, event | category | flops | bytes accessed | tf_op | source)
XLA Modules:
  0.0 62.3 jit_solution(15876749319634047222)
XLA Ops:
  0.0 60.6 %march.1 = bf16[4,256,128]{2,1,0:T(8,128)(2,1)} custom-call(bf16[15,256,1280]{2,1,0:T(8,128)(2,1)} %w_hbm.1, bf16[15,256,128]{2,1,0:T(8,128)(2,1)} %h_hbm.1, bf16[256,256]{1,0:T(8,128)(2,1)} %inv_hbm.1, s32[1,10]{1,0:T(1,128)} %range_ref.1, s32[1,256]{1,0:T(1,128)} %bitcast.2, s32[1,256]{1,0:T(1,128)} %bitcast.3, bf16[256,4,128]{2,1,0:T(4,128)(2,1)} %resid_hbm.1), custom_call_target="tpu_custom_call" | custom-call | tf_op jit(solution)/shard_map/march/pallas_call | solution.py:507
  60.6 1.7 %copy.9 = bf16[4,256,128]{2,1,0:T(8,128)(2,1)} copy(bf16[4,256,128]{2,1,0:T(8,128)(2,1)} %march.1) | data formatting | bytes 524288

commit v3 on v2

--- a/solution.py
+++ b/solution.py
@@ -164,9 +164,21 @@
     def rim_copy(first, count, at):
         return remote(h_buf.at[pl.ds(band - rim + first, count)], rim_buf.at[pl.ds(first, count)], rim_ss.at[at], rim_rs.at[at], t, lag_at(1))
 
-    def turn_rim(q):
-        before = rim_buf[q].T
-        ht[pl.ds((band + rim - 1 - q) * shots, shots), :] = jnp.where(is_first, jnp.zeros_like(before), before)
+    def rim_start(first, count, at):
+        pl.when(l != lags - 1)(rim_copy(first, count, at).start)
+
+    def rim_take(first, count, at):
+        rows = pl.ds((band + rim - first - count) * shots, count * shots)
+
+        @pl.when(is_first)
+        def _():
+            ht[rows, :] = jnp.zeros((count * shots, width), BF16)
+
+        @pl.when(l != 0)
+        def _():
+            landed(rim_buf.at[pl.ds(first, count)], rim_rs.at[at])
+            for q in range(first, first + count):
+                ht[pl.ds((band + rim - 1 - q) * shots, shots), :] = rim_buf[q].T
 
     def slots(p):
         return pl.ds(pl.multiple_of(p * CAP, CAP), CAP)
@@ -274,7 +286,7 @@
         pl.semaphore_wait(barrier, jnp.where(is_first, lags - 1 + patches - 1 + 4 * (lags - 1), lags - 1 + patches - 1 + 4))
     with jax.named_scope("pair0"):
         pair_copy(0, 1, 0).start()
-        rim_copy(rim - 1, 1, 0).start()
+        rim_start(rim - 1, 1, 0)
 
     with jax.named_scope("prep"):
         recv = tile_ref.shape[1]
@@ -301,20 +313,18 @@
         src_out[...] = dot_rows(placer, mine).astype(BF16)
         src_in[own_slots, :] = src_out[own_slots, :]
 
-    with jax.named_scope("src0"):
-        lax.fori_loop(1, patches, src_start, 0)
     with jax.named_scope("pairwait0"):
         pair_wait(0, 1)
     with jax.named_scope("send0"):
         send_step(0)
-        rim_copy(0, rim - 1, 1).start()
+        lax.fori_loop(1, patches, src_start, 0)
+        rim_start(0, rim - 1, 1)
     with jax.named_scope("later2"):
         set_lag(rim, shots, (steps - 1) * shots)
         lax.fori_loop(rim + 1, band, later_steps, 0)
 
     with jax.named_scope("rim1"):
-        rim_copy(rim - 1, 1, 0).wait()
-        turn_rim(rim - 1)
+        rim_take(rim - 1, 1, 0)
         lax.fori_loop(0, rim, second_step_rim, 0)
         pair_copy(1, 1, 1).start()
 
@@ -326,24 +336,18 @@
         onto = (labels == (iota((patches * CAP, width), 1) + 1).astype(F32)).astype(BF16)
         source[...] = dot_rows(src_in[...], onto)
 
+    with jax.named_scope("rs0"):
+        pieces(0)
     with jax.named_scope("send1"):
         pair_wait(1, 1)
         send_step(1)
-    with jax.named_scope("rs0"):
-        pieces(0)
-    with jax.named_scope("rimwait"):
-        rim_copy(0, rim - 1, 1).wait()
     with jax.named_scope("rim23"):
-        for q in range(rim - 1):
-            turn_rim(q)
+        rim_take(0, rim - 1, 1)
         lax.fori_loop(0, rim, last_steps_rim, 0)
         pair_copy(2, steps - 2, 2).start()
-    with jax.named_scope("send23"):
+    with jax.named_scope("send2"):
         pair_wait(2, steps - 2)
-        for s in range(2, steps):
-            send_step(s)
-    with jax.named_scope("rs1"):
-        pieces(1)
+        send_step(2)
 
     def place_of(i):
         return HALF * 2 if i == HALF else i - (i > HALF)
@@ -406,6 +410,8 @@
 
     @pl.when(is_first)
     def _():
+        with jax.named_scope("rs1"):
+            pieces(1)
         with jax.named_scope("p0"):
             piece_wait(0)
         with jax.named_scope("terms1"):
@@ -417,8 +423,8 @@
             older_terms(0)
         with jax.named_scope("rs2"):
             pieces(2)
-        with jax.named_scope("rs3"):
-            own_last[...] = last_sum()
+        with jax.named_scope("send3"):
+            send_step(last)
         for n in range(1, last):
             with jax.named_scope(f"p{n}"):
                 piece_wait(n)
@@ -428,20 +434,32 @@
                 with jax.named_scope(f"terms{n + 1}{g}"):
                     send_terms(n + 1, g)
             spread(n)
-            with jax.named_scope(f"older{n + 1}"):
-                older_terms(n)
+            if n == 1:
+                with jax.named_scope("older2"):
+                    older_terms(n)
+                with jax.named_scope("rs3"):
+                    own_last[...] = last_sum()
 
     @pl.when(l != 0)
     def _():
+        def pass_on(n):
+            landed(dens.at[n, own_shots], sp_rs.at[n])
+            for d in range(1, lags):
+                others(d)(ag_copy(n, d, pass_ss).start)
+
+        with jax.named_scope("rs1"):
+            pieces(1)
         with jax.named_scope("rs2"):
             pieces(2)
+        with jax.named_scope("sp0"):
+            pass_on(0)
+        with jax.named_scope("send3"):
+            send_step(last)
         with jax.named_scope("rs3"):
             own_last[...] = last_sum()
         with jax.named_scope("sp"):
-            for n in range(last):
-                landed(dens.at[n, own_shots], sp_rs.at[n])
-                for d in range(1, lags):
-                    others(d)(ag_copy(n, d, pass_ss).start)
+            for n in range(1, last):
+                pass_on(n)
 
     with jax.named_scope("nblast"):
         rest = -nb_sum(own_last[...])
@@ -476,6 +494,12 @@
         for s in range(steps):
             out_ref[s] = dens[s].T
         landed(src_in.at[pl.ds(0, (patches - 1) * CAP)], src_ss)
+
+        @pl.when(l != lags - 1)
+        def _():
+            landed(rim_buf.at[pl.ds(rim - 1, 1)], rim_ss.at[0])
+            landed(rim_buf.at[pl.ds(0, rim - 1)], rim_ss.at[1])
+
         landed(rbuf.at[:, pl.ds(0, lags - 1)], rs_ss)
         landed(got, pair_ss)
         landed(nbuf, nb_ss)

time: 62.4 us -> 61 us (0.978); the launches traced: 62.3 us -> 60 us
  Pallas kernels: 60.6 us -> 58.3 us
    pallas_call x1, Pallas kernels: 60.6 us -> 58.3 us  [local(): pl.pallas_call(functools.partial(kernel, patches, lags), out_shape=jax.Sh...]
where the time goes in v3:
time: 61 us; the launch traced here: 60 us
  Pallas kernels  58.3 us (96%)
  local copies, waits for them, and re-layouts  1.67 us (3%)
    pallas_call x1, Pallas kernels, local(): pl.pallas_call(functools.partial(kernel, patches, lags), out_shape=jax.Sh...  58.3 us
    unnamed x1, local copies, waits for them, and re-layouts  1.67 us

profile of v3, /device:TPU:1, one launch (start us, length us, event | category | flops | bytes accessed | tf_op | source)
XLA Modules:
  0.0 60.0 jit_solution(11046773411785794755)
XLA Ops:
  0.0 58.3 %march.1 = bf16[4,256,128]{2,1,0:T(8,128)(2,1)} custom-call(bf16[15,256,1280]{2,1,0:T(8,128)(2,1)} %w_hbm.1, bf16[15,256,128]{2,1,0:T(8,128)(2,1)} %h_hbm.1, bf16[256,256]{1,0:T(8,128)(2,1)} %inv_hbm.1, s32[1,10]{1,0:T(1,128)} %range_ref.1, s32[1,256]{1,0:T(1,128)} %bitcast.2, s32[1,256]{1,0:T(1,128)} %bitcast.3, bf16[256,4,128]{2,1,0:T(4,128)(2,1)} %resid_hbm.1), custom_call_target="tpu_custom_call" | custom-call | tf_op jit(solution)/shard_map/march/pallas_call | solution.py:531
  58.4 1.7 %copy.9 = bf16[4,256,128]{2,1,0:T(8,128)(2,1)} copy(bf16[4,256,128]{2,1,0:T(8,128)(2,1)} %march.1) | data formatting | bytes 524288

commit v4 on v3

--- a/solution.py
+++ b/solution.py
@@ -433,12 +433,13 @@
                     finish(n, g)
                 with jax.named_scope(f"terms{n + 1}{g}"):
                     send_terms(n + 1, g)
+                if n == last - 1 and g == 0:
+                    with jax.named_scope("rs3"):
+                        own_last[...] = last_sum()
             spread(n)
             if n == 1:
                 with jax.named_scope("older2"):
                     older_terms(n)
-                with jax.named_scope("rs3"):
-                    own_last[...] = last_sum()
 
     @pl.when(l != 0)
     def _():
@@ -451,10 +452,10 @@
             pieces(1)
         with jax.named_scope("rs2"):
             pieces(2)
+        with jax.named_scope("send3"):
+            send_step(last)
         with jax.named_scope("sp0"):
             pass_on(0)
-        with jax.named_scope("send3"):
-            send_step(last)
         with jax.named_scope("rs3"):
             own_last[...] = last_sum()
         with jax.named_scope("sp"):

time: 61 us -> 60.4 us (level); the launches traced: 60 us -> 60.3 us
  no operation moved by 1% of the time
where the time goes in v4:
time: 60.4 us; the launch traced here: 60.3 us
  Pallas kernels  58.6 us (97%)
  local copies, waits for them, and re-layouts  1.67 us (3%)
    pallas_call x1, Pallas kernels, local(): pl.pallas_call(functools.partial(kernel, patches, lags), out_shape=jax.Sh...  58.6 us
    unnamed x1, local copies, waits for them, and re-layouts  1.67 us

profile of v4, /device:TPU:1, one launch (start us, length us, event | category | flops | bytes accessed | tf_op | source)
XLA Modules:
  0.0 60.3 jit_solution(4123658177420752359)
XLA Ops:
  0.0 58.6 %march.1 = bf16[4,256,128]{2,1,0:T(8,128)(2,1)} custom-call(bf16[15,256,1280]{2,1,0:T(8,128)(2,1)} %w_hbm.1, bf16[15,256,128]{2,1,0:T(8,128)(2,1)} %h_hbm.1, bf16[256,256]{1,0:T(8,128)(2,1)} %inv_hbm.1, s32[1,10]{1,0:T(1,128)} %range_ref.1, s32[1,256]{1,0:T(1,128)} %bitcast.2, s32[1,256]{1,0:T(1,128)} %bitcast.3, bf16[256,4,128]{2,1,0:T(4,128)(2,1)} %resid_hbm.1), custom_call_target="tpu_custom_call" | custom-call | tf_op jit(solution)/shard_map/march/pallas_call | solution.py:532
  58.6 1.7 %copy.9 = bf16[4,256,128]{2,1,0:T(8,128)(2,1)} copy(bf16[4,256,128]{2,1,0:T(8,128)(2,1)} %march.1) | data formatting | bytes 524288
